TPU v7x, 128 devices: a whole 4x4x4 slice. The times are simulated.
128 devices in a mesh: dp: 16 (over y_hi, z, core), tensor: 8 (over y_lo, x).
Axes of the slice: x: 4, y: 4 (y_hi: 2, y_lo: 2; y = y_hi * 2 + y_lo), z: 4, core: 2. Of those that a mesh axis runs over, the one named last changes fastest.
Arguments:
- saved_queries: bfloat16 [16384, 8192], P('dp', 'tensor'), may hold values from -200 to 200
- saved_keys: bfloat16 [16384, 1024], P('dp', 'tensor'), may hold values from -200 to 200
- saved_values: bfloat16 [16384, 1024], P('dp', 'tensor'), may hold values from -6 to 6
- out_grad: bfloat16 [16384, 8192], P(('dp', 'tensor')), may hold values from -2.5 to 2.5
- act_exponent: int32 [1], replicated, may hold values from -6 to 3
- grad_exponent: int32 [1], replicated, may hold values from -4 to 1
Outputs:
- grad_weight: float32 [8192, 8192], P('dp', 'tensor')
All inputs are finite; a program needn't handle non-finite values.
Results may differ from a plain program's by a relative error of at most 0.012.
Values may be sent and summed in bfloat16 or wider, within the bound.
A program may use at most 128 MiB of HBM per device.

v0:
```python
import jax
import jax.numpy as jnp
from jax import lax
from jax.sharding import PartitionSpec as P

HEAD_DIM = 128


SATURATION = 448.0


def quantize(values_in, exponent):
    factor = SATURATION * jnp.exp2(-exponent[0].astype(jnp.float32))
    return jnp.clip(values_in * factor, -SATURATION, SATURATION).astype(jnp.bfloat16)


def attend(query_rows, key_rows, value_rows):
    scores = jnp.dot(query_rows, key_rows.T, preferred_element_type=jnp.float32) * HEAD_DIM ** (
        -0.5
    )
    positions = jnp.arange(query_rows.shape[0], dtype=jnp.int32)
    causal = positions[None, :] <= positions[:, None]
    scores = jnp.where(causal, scores, jnp.float32(-1e30))
    row_max = jnp.max(scores, axis=1, keepdims=True)
    weights = jnp.exp(scores - row_max)
    probabilities = (weights / jnp.sum(weights, axis=1, keepdims=True)).astype(jnp.bfloat16)
    return jnp.dot(probabilities, value_rows, preferred_element_type=jnp.float32)


def on_device(saved_queries, saved_keys, saved_values, out_grad, act_exponent, grad_exponent):
    seq_len = saved_queries.shape[0]
    local_width = saved_queries.shape[1]
    heads_here = local_width // HEAD_DIM
    dequant = jnp.exp2((act_exponent[0] + grad_exponent[0]).astype(jnp.float32)) / (
        SATURATION * SATURATION
    )

    def one_head(head_index, scaled_rows):
        query_rows = lax.dynamic_slice_in_dim(saved_queries, head_index * HEAD_DIM, HEAD_DIM, 1)
        attended = attend(query_rows, saved_keys, saved_values)
        return lax.dynamic_update_slice_in_dim(
            scaled_rows, quantize(attended, act_exponent), head_index * HEAD_DIM, 1
        )

    act_scaled = lax.fori_loop(
        0, heads_here, one_head, jnp.zeros((seq_len, local_width), jnp.bfloat16)
    )
    grad_scaled = quantize(out_grad.astype(jnp.float32), grad_exponent)
    running = lax.dot_general(
        lax.all_gather(grad_scaled, "tensor", axis=0, tiled=True),
        act_scaled,
        (((0,), (0,)), ((), ())),
        preferred_element_type=jnp.float32,
    )
    grad_weight = lax.psum_scatter(
        (running * dequant).astype(jnp.bfloat16), "dp", scatter_dimension=0, tiled=True
    ).astype(jnp.float32)
    return grad_weight


def solution(mesh):
    in_specs = (
        P("dp", "tensor"),
        P("dp", "tensor"),
        P("dp", "tensor"),
        P(("dp", "tensor"), None),
        P(),
        P(),
    )
    out_specs = P("dp", "tensor")
    return jax.shard_map(
        on_device, mesh=mesh, in_specs=in_specs, out_specs=out_specs, check_vma=False
    )
```

profile of v0, /device:TPU:0, one launch (start us, length us, event | category | flops | bytes accessed | tf_op | source)
XLA Modules:
  0.0 367.2 jit_solution(14772406896722090747)
XLA Ops:
  6.5 0.0 all-gather.2.cloned.1.call-start
  7.2 0.0 copy-start
  7.2 0.0 copy-start.1
  7.3 3.5 clamp_convert_fusion
  10.7 0.0 all-gather.2.cloned.1.call-update
  10.8 0.0 reduce-scatter.2.cloned.1.call-start
  11.6 0.3 broadcast_in_dim.25
  11.8 0.0 copy-done
  11.8 0.0 copy-done.1
  11.8 25.3 %while.15 = (s32[]{:T(128)}, bf16[1024,1024]{1,0:T(8,128)(2,1)S(1)}, bf16[1024,1024]{1,0:T(8,128)(2,1)}, bf16[1024,128]{1,0:T(8,128)(2,1)S(1)}, bf16[1024,128]{1...) while((s32[]{:T(128)}, bf16[1024,1024]{1,0:T(8,128)(2,1)S(1)}, ...), condition=%wide.region_3.4_spmd, body=%wide.region_0.3_spmd.sunk | while | flops 552990720 | bytes 13652127 | solution.py:45
  11.9 1.7 fusion.23
  13.5 0.5 fusion.24
  14.1 0.9 fusion.25
  15.0 1.7 fusion.23
  16.7 0.5 fusion.24
  17.2 0.9 fusion.25
  18.2 1.7 fusion.23
  19.8 0.5 fusion.24
  20.4 0.9 fusion.25
  21.3 1.7 fusion.23
  23.0 0.5 fusion.24
  23.6 0.9 fusion.25
  24.5 1.7 fusion.23
  26.2 0.5 fusion.24
  26.7 0.9 fusion.25
  27.7 1.7 fusion.23
  29.3 0.5 fusion.24
  29.9 0.9 fusion.25
  30.8 1.7 fusion.23
  32.5 0.5 fusion.24
  33.0 0.9 fusion.25
  34.0 1.7 fusion.23
  35.7 0.5 fusion.24
  36.2 0.9 fusion.25
  37.1 146.7 %all-gather.2.cloned.1.call-done = bf16[1024,8192]{1,0:T(8,128)(2,1)} async-done(((bf16[128,8192]{1,0:T(8,128)(2,1)}), bf16[1024,8192]{1,0:T(8,128)(2,1)}) %all-gather.2.cloned.1.call-update) | async-done | bytes 16777232 | tf_op jit(solution)/shard_map/all_gather | solution.py:50
  183.9 27.4 %multiply_convert_fusion = bf16[8192,1024]{1,0:T(8,128)(2,1)} fusion(bf16[1024,8192]{1,0:T(8,128)(2,1)} %all-gather.2.cloned.1.call-done, bf16[1024,1024]{1,0:T(8,128)(2,1)S(1)} %get-tuple-element.158, f32[]{:T(128)} %bitcast.2), kind=kOutput, calls=%fused_computation.16 | convolution fusion | flops 17196646400 | bytes 35651588 | tf_op jit(solution)/shard_map/dot_general | solution.py:49
  211.3 0.0 reduce-scatter.2.cloned.1.call-update
  211.3 146.3 %reduce-scatter.2.cloned.1.call-done = bf16[512,1024]{1,0:T(8,128)(2,1)} async-done(((bf16[8192,1024]{1,0:T(8,128)(2,1)}), bf16[512,1024]{1,0:T(8,128)(2,1)}) %reduce-scatter.2.cloned.1.call-update) | async-done | bytes 1048592 | tf_op jit(solution)/shard_map/reduce_scatter | solution.py:55
  357.6 2.8 convert_element_type.54
Async XLA Ops:
  6.5 177.3 %all-gather.2.cloned.1.call-start = ((), (), s32[]{:S(2)}) async-start(), calls=%async_computation.1 | async-start | bytes 18874368 | tf_op jit(solution)/shard_map/all_gather | solution.py:50
  7.2 4.6 %copy-start = (bf16[1024,128]{1,0:T(8,128)(2,1)S(1)}, bf16[1024,128]{1,0:T(8,128)(2,1)}, u32[]{:S(2)}) copy-start(bf16[1024,128]{1,0:T(8,128)(2,1)} %param.9) | copy-start | bytes 786436
  7.2 4.6 %copy-start.1 = (bf16[1024,128]{1,0:T(8,128)(2,1)S(1)}, bf16[1024,128]{1,0:T(8,128)(2,1)}, u32[]{:S(2)}) copy-start(bf16[1024,128]{1,0:T(8,128)(2,1)} %param.10) | copy-start | bytes 786436
  10.8 346.8 %reduce-scatter.2.cloned.1.call-start = ((), (), s32[]{:S(2)}) async-start(), calls=%async_computation.2 | async-start | bytes 17825792 | tf_op jit(solution)/shard_map/reduce_scatter | solution.py:55
Sparse Core Ops, SparseCore 0:
  10.9 172.9 all-gather.1
  211.4 146.1 reduce-scatter.1
where the time goes:
time: 368 us; the launch traced here: 367 us
  waiting for transfers between devices  293 us (80%)
  matrix products  48.3 us (13%)
  between operations  14.9 us (4%)
  other arithmetic  10.5 us (3%)
    all_gather x1, waiting for transfers between devices, on_device(): lax.all_gather(grad_scaled, 'tensor', axis=0, tiled=True)  147 us
    reduce_scatter x1, waiting for transfers between devices, on_device(): lax.psum_scatter((running * dequant).astype(jnp.bfloat16), 'dp', scatter_...  146 us
    dot_general x1, matrix products, on_device(): lax.dot_general(lax.all_gather(grad_scaled, 'tensor', axis=0, tiled=True)...  27.4 us
    dot_general x8, matrix products, attend(): jnp.dot(query_rows, key_rows.T, preferred_element_type=jnp.float32)  13.4 us
    dot_general x8, matrix products, attend(): jnp.dot(probabilities, value_rows, preferred_element_type=jnp.float32)  7.5 us
  transfers between devices with their start and end apart: 2, of which 2 were waited for; matrix products, arithmetic and copies ran while one was open for 7% of the time, Pallas kernels for 0%

commit v1 on v0

v1 whole, which is shorter than its diff:
```python
import math

import jax
import jax.numpy as jnp
from jax import lax
from jax.experimental import pallas as pl
from jax.experimental.pallas import tpu as pltpu
from jax.sharding import PartitionSpec as P

MESH = pl.DeviceIdType.MESH
SATURATION = 448.0
HEAD_DIM = 128
EXPONENT_SCALE = HEAD_DIM**-0.5 * math.log2(math.e)
BF16, F32 = jnp.bfloat16, jnp.float32
VMEM_LIMIT = 67_043_328

OWN = 0
OTHER = 1


def schedule():
    steps = [("mm", 0, OWN, 0), ("mm", 0, OWN, 1)]
    for o in range(1, 8):
        steps.append(("ring", o + 1))
        steps += [("mm", o, OWN, 0), ("mm", o, OWN, 1)]
        if o == 3:
            steps.append(("attended", 0))
        if o == 4:
            steps += [("mm", k, OTHER, 0) for k in range(5)]
        if o in (5, 6):
            steps.append(("mm", o, OTHER, 0))
        if o == 6:
            steps.append(("attended", 1))
            steps += [("mm", k, OTHER, 1) for k in range(7)]
    steps += [("mm", 7, OTHER, 0), ("mm", 7, OTHER, 1)]
    return steps


def kernel(q_hbm, k_hbm, v_hbm, g_hbm, ae_ref, ge_ref, out_ref,
           q_ref, k_ref, v_ref, g_in, vt_ref, g_send, g_all, at_own, at_oth,
           z2_send, z2_recv, zf_send, zf_recv, y_send, y_recv, kept,
           in_sem, s1_send, s1_recv, x_send, x_recv, xf_send, xf_recv, a_send, a_recv,
           z2_ssem, z2_rsem, zf_ssem, zf_rsem, y_ssem, y_rsem):
    d = lax.axis_index("dp")
    t = lax.axis_index("tensor")
    yh, z, c = lax.div(d, 8), lax.rem(lax.div(d, 2), 4), lax.rem(d, 2)
    low, x = lax.div(t, 4), lax.rem(t, 4)
    partner_dp = d + 1 - 2 * c
    side_t = (1 - low) * 4 + x
    far_dp = (1 - yh) * 8 + z * 2 + c
    x_up, x_down = lax.rem(x + 1, 4), lax.rem(x + 3, 4)
    z_up, z_down = lax.rem(z + 1, 4), lax.rem(z + 3, 4)

    def dev(dp, tensor):
        return {"dp": dp, "tensor": tensor}

    core_dev, side_dev, cross_dev = dev(partner_dp, t), dev(d, side_t), dev(partner_dp, side_t)
    xp_dev, xm_dev = dev(d, low * 4 + x_up), dev(d, low * 4 + x_down)
    zp_dev, zm_dev = dev(yh * 8 + z_up * 2 + c, t), dev(yh * 8 + z_down * 2 + c, t)
    far_dev, far_side_dev = dev(far_dp, t), dev(far_dp, side_t)
    quarter_dev = (core_dev, side_dev, cross_dev)
    quarter_slot = ((1 - c, low), (c, 1 - low), (1 - c, 1 - low))

    def remote(src, dst, ssem, rsem, to):
        return pltpu.make_async_remote_copy(
            src_ref=src, dst_ref=dst, send_sem=ssem, recv_sem=rsem, device_id=to, device_id_type=MESH
        )

    loads = [
        pltpu.make_async_copy(src, dst, in_sem.at[i])
        for i, (src, dst) in enumerate(((g_hbm, g_in), (k_hbm, k_ref), (v_hbm, v_ref), (q_hbm, q_ref)))
    ]
    for load in loads:
        load.start()
    barrier = pltpu.get_barrier_semaphore()
    for to in (core_dev, side_dev, cross_dev, xp_dev, xm_dev, zp_dev, zm_dev, far_dev, far_side_dev):
        pl.semaphore_signal(barrier, inc=1, device_id=to, device_id_type=MESH)

    grad_factor = SATURATION * jnp.exp2(jnp.full((1, 256), -ge_ref[0], jnp.int32).astype(F32))
    act_factor = SATURATION * jnp.exp2(jnp.full((1, 256), -ae_ref[0], jnp.int32).astype(F32))
    dequant = jnp.exp2(jnp.full((1, 256), ae_ref[0] + ge_ref[0], jnp.int32).astype(F32)) / (
        SATURATION * SATURATION
    )

    def block_of(o):
        role = lax.div(o, 2)
        shift = jnp.where(role == 0, 2, jnp.where(role == 1, 1, jnp.where(role == 2, 3, 0)))
        to_z = lax.rem(z + shift, 4)
        to_yh = jnp.where(lax.rem(o, 2) == 0, 1 - yh, yh)
        return to_yh * 16 + to_z * 4

    def s1_copy(k, o):
        return remote(g_send.at[k, o], g_all.at[o, c, low, x], s1_send.at[k, o], s1_recv.at[k, o], quarter_dev[k])

    def s1_wait(k, o):
        s, l = quarter_slot[k]
        remote(g_send.at[k, o], g_all.at[o, s, l, x], s1_send.at[k, o], s1_recv.at[k, o], quarter_dev[k]).wait_recv()

    loads[0].wait()

    def scaled(block):
        values = g_in[:, pl.ds(pl.multiple_of(block * 256, 256), 256)].astype(F32)
        return jnp.clip(values * grad_factor, -SATURATION, SATURATION).astype(BF16)

    def quantize_block(o, carry):
        base = block_of(o)
        g_send[1, o] = scaled(base + 2 * c + 1 - low)
        g_send[2, o] = scaled(base + 2 * (1 - c) + 1 - low)
        g_send[0, o] = scaled(base + 2 * (1 - c) + low)
        g_all[o, c, low, x] = scaled(base + 2 * c + low)
        return carry

    lax.fori_loop(0, 8, quantize_block, 0)
    pl.semaphore_wait(barrier, 9)

    def send_block(o, carry):
        for k in (1, 2, 0):
            s1_copy(k, o).start()
        return carry

    lax.fori_loop(0, 8, send_block, 0)

    def x_copy(o, i):
        src = g_all.at[o, :, :, x]
        return remote(src, src, x_send.at[i, o], x_recv.at[i, o], (xp_dev, xm_dev)[i])

    def x_arrival(o, i):
        src = g_all.at[o, :, :, (x_down, x_up)[i]]
        return remote(src, src, x_send.at[i, o], x_recv.at[i, o], (xp_dev, xm_dev)[i])

    def xf_copy(o, i):
        src = g_all.at[o, i, :, (x_down, x_up)[i]]
        return remote(src, src, xf_send.at[i, o], xf_recv.at[i, o], (xp_dev, xm_dev)[i])

    def xf_arrival(o, i):
        src = g_all.at[o, i, :, lax.rem(x + 2, 4)]
        return remote(src, src, xf_send.at[i, o], xf_recv.at[i, o], (xp_dev, xm_dev)[i])

    def ring_start(o):
        for k in range(3):
            s1_wait(k, o)
        for i in range(2):
            x_copy(o, i).start()

    def ring_forward(o):
        for i in range(2):
            x_arrival(o, i).wait_recv()
            xf_copy(o, i).start()

    def a_rows(half):
        return pl.ds(pl.multiple_of(half * 512, 512), 512)

    def a_copy(half, i):
        src = at_own.at[c, a_rows(half)]
        dst = at_own.at[c, a_rows(half)] if i == 0 else at_oth.at[c, a_rows(half)]
        return remote(src, dst, a_send.at[i, half], a_recv.at[i, half], (core_dev, side_dev)[i])

    def a_forward(half):
        src = at_oth.at[c, a_rows(half)]
        return remote(src, src, a_send.at[2, half], a_recv.at[2, half], core_dev)

    def a_wait(half, i):
        ref = at_own.at[1 - c, a_rows(half)] if i == 0 else at_oth.at[c if i == 1 else 1 - c, a_rows(half)]
        remote(ref, ref, a_send.at[i, half], a_recv.at[i, half], (core_dev, side_dev, core_dev)[i]).wait_recv()

    for load in loads[1:]:
        load.wait()
    vt_ref[...] = v_ref[...].astype(F32).T.astype(BF16)
    causal = lax.broadcasted_iota(jnp.int32, (256, 256), 0) <= lax.broadcasted_iota(jnp.int32, (256, 256), 1)

    def head(index):
        columns = pl.ds(pl.multiple_of(index * HEAD_DIM, HEAD_DIM), HEAD_DIM)
        for tb in range(4):
            rows = slice(tb * 256, (tb + 1) * 256)
            query = q_ref[rows, columns]

            def scores_of(keys):
                return lax.dot_general(keys, query, (((1,), (1,)), ((), ())), preferred_element_type=F32)

            last = jnp.where(causal, scores_of(k_ref[rows, :]), F32(-1e30))
            top = jnp.max(last, axis=0, keepdims=True)
            if tb > 0:
                early = scores_of(k_ref[: tb * 256, :])
                top = jnp.maximum(top, jnp.max(early, axis=0, keepdims=True))
            weights = jnp.exp2((last - top) * EXPONENT_SCALE)
            total = jnp.sum(weights, axis=0, keepdims=True)
            value = jnp.dot(vt_ref[:, rows], weights.astype(BF16), preferred_element_type=F32)
            if tb > 0:
                weights = jnp.exp2((early - top) * EXPONENT_SCALE)
                total += jnp.sum(weights, axis=0, keepdims=True)
                value += jnp.dot(vt_ref[:, : tb * 256], weights.astype(BF16), preferred_element_type=F32)
            value = jnp.clip(value * (act_factor / total), -SATURATION, SATURATION).astype(BF16)
            at_own[c, columns, rows] = value

    def two_heads(i, carry):
        head(2 * i)
        head(2 * i + 1)

        @pl.when(i >= 2)
        def _():
            ring_forward(i - 2)

        ring_start(i)

        @pl.when(lax.rem(i, 2) == 1)
        def _():
            half = lax.div(i, 2)
            a_copy(half, 0).start()
            a_copy(half, 1).start()

        return carry

    lax.fori_loop(0, 4, two_heads, 0)

    def z2_copy(stream, half):
        return remote(z2_send.at[stream, half], z2_recv.at[stream, half], z2_ssem.at[stream, half],
                      z2_rsem.at[stream, half], (zp_dev, zm_dev)[half])

    def zf_copy(way, stream, half):
        return remote(zf_send.at[way, stream, half], zf_recv.at[way, stream, half], zf_ssem.at[way, stream, half],
                      zf_rsem.at[way, stream, half], (zp_dev, zm_dev)[way])

    def y_copy(k, half):
        return remote(y_send.at[k, half], y_recv.at[k, half], y_ssem.at[k, half], y_rsem.at[k, half],
                      (far_dev, side_dev, far_side_dev)[k])

    have = set()

    def need(key, wait):
        if key not in have:
            have.add(key)
            wait()

    def multiply(o, which, half):
        for i in range(2):
            need(("x", o, i), lambda: x_arrival(o, i).wait_recv())
            need(("xf", o, i), lambda: xf_arrival(o, i).wait_recv())
        if which == OWN:
            need(("a0", half), lambda: a_wait(half, 0))
        else:
            need(("a2", half), lambda: a_wait(half, 2))
        role, far = o // 2, o % 2 == 0
        stream = 2 * (o % 2) + which
        adds, copy = [], None
        if role == 0:
            dst, copy = z2_send.at[stream, half], z2_copy(stream, half)
        elif role < 3:
            way = role - 1
            dst, copy = zf_send.at[way, stream, half], zf_copy(way, stream, half)
            if way == half:
                z2_copy(stream, half).wait_recv()
                adds = [z2_recv.at[stream, half]]
        else:
            for way in range(2):
                zf_copy(way, stream, half).wait_recv()
            adds = [zf_recv.at[way, stream, half] for way in range(2)]
            if which == OWN and not far:
                dst = kept.at[half]
            else:
                k = 0 if which == OWN else (2 if far else 1)
                dst, copy = y_send.at[k, half], y_copy(k, half)
        at = (at_own, at_oth)[which]

        def tile(n, carry):
            rows = pl.ds(pl.multiple_of(half * 512 + n * 256, 256), 256)
            part = pl.ds(pl.multiple_of(n * 256, 256), 256)
            total = jnp.dot(at[0, rows, :], g_all[o, 0].reshape(1024, 256), preferred_element_type=F32)
            total += jnp.dot(at[1, rows, :], g_all[o, 1].reshape(1024, 256), preferred_element_type=F32)
            for add in adds:
                total += add[part, :].astype(F32)
            dst[part, :] = total.astype(BF16)
            return carry

        lax.fori_loop(0, 2, tile, 0)
        if copy is not None:
            copy.start()

    ring_forwarded, ring_started = 2, 4
    for step in schedule():
        if step[0] == "ring":
            if ring_forwarded < 8:
                for i in range(2):
                    x_arrival(ring_forwarded, i).wait_recv()
                    xf_copy(ring_forwarded, i).start()
                ring_forwarded += 1
            if ring_started < 8:
                ring_start(ring_started)
                ring_started += 1
            have.update(("x", o, i) for o in range(ring_forwarded) for i in range(2))
        elif step[0] == "attended":
            a_wait(step[1], 1)
            a_forward(step[1]).start()
        else:
            have.update(("x", o, i) for o in range(2) for i in range(2))
            multiply(*step[1:])

    for half in range(2):
        rows = slice(half * 512, (half + 1) * 512)
        for k in range(3):
            y_copy(k, half).wait_recv()
        mine = kept[half].astype(F32) + y_recv[0, half].astype(F32)
        out_ref[rows, pl.ds(pl.multiple_of(low * 256, 256), 256)] = mine * dequant
        theirs = y_recv[1, half].astype(F32) + y_recv[2, half].astype(F32)
        out_ref[rows, pl.ds(pl.multiple_of((1 - low) * 256, 256), 256)] = theirs * dequant

    def drain(o, carry):
        for k in range(3):
            s1_copy(k, o).wait_send()
        for i in range(2):
            x_copy(o, i).wait_send()
            xf_copy(o, i).wait_send()
        return carry

    lax.fori_loop(0, 8, drain, 0)
    for half in range(2):
        a_copy(half, 0).wait_send()
        a_copy(half, 1).wait_send()
        a_forward(half).wait_send()
        for k in range(3):
            y_copy(k, half).wait_send()
        for stream in range(4):
            z2_copy(stream, half).wait_send()
            for way in range(2):
                zf_copy(way, stream, half).wait_send()


def on_device(queries, keys, values, out_grad, act_exponent, grad_exponent):
    anywhere = pl.BlockSpec(memory_space=pl.ANY)
    scalar = pl.BlockSpec(memory_space=pltpu.SMEM)
    dma = pltpu.SemaphoreType.DMA
    transposed = pl.pallas_call(
        kernel,
        name="project_grad",
        out_shape=jax.ShapeDtypeStruct((1024, 512), F32),
        in_specs=[anywhere] * 4 + [scalar] * 2,
        out_specs=pl.BlockSpec(memory_space=pltpu.VMEM),
        scratch_shapes=[
            pltpu.VMEM((1024, 1024), BF16),
            pltpu.VMEM((1024, 128), BF16),
            pltpu.VMEM((1024, 128), BF16),
            pltpu.VMEM((128, 8192), BF16),
            pltpu.VMEM((128, 1024), BF16),
            pltpu.VMEM((3, 8, 128, 256), BF16),
            pltpu.VMEM((8, 2, 2, 4, 128, 256), BF16),
            pltpu.VMEM((2, 1024, 1024), BF16),
            pltpu.VMEM((2, 1024, 1024), BF16),
            pltpu.VMEM((4, 2, 512, 256), BF16),
            pltpu.VMEM((4, 2, 512, 256), BF16),
            pltpu.VMEM((2, 4, 2, 512, 256), BF16),
            pltpu.VMEM((2, 4, 2, 512, 256), BF16),
            pltpu.VMEM((3, 2, 512, 256), BF16),
            pltpu.VMEM((3, 2, 512, 256), BF16),
            pltpu.VMEM((2, 512, 256), BF16),
            dma((4,)),
            dma((3, 8)), dma((3, 8)),
            dma((2, 8)), dma((2, 8)),
            dma((2, 8)), dma((2, 8)),
            dma((3, 2)), dma((3, 2)),
            dma((4, 2)), dma((4, 2)),
            dma((2, 4, 2)), dma((2, 4, 2)),
            dma((3, 2)), dma((3, 2)),
        ],
        compiler_params=pltpu.CompilerParams(
            collective_id=0, has_side_effects=True, vmem_limit_bytes=VMEM_LIMIT
        ),
    )(queries, keys, values, out_grad, act_exponent, grad_exponent)
    return transposed.T


def solution(mesh):
    in_specs = (
        P("dp", "tensor"),
        P("dp", "tensor"),
        P("dp", "tensor"),
        P(("dp", "tensor"), None),
        P(),
        P(),
    )
    return jax.shard_map(
        on_device, mesh=mesh, in_specs=in_specs, out_specs=P("dp", "tensor"), check_vma=False
    )
```

time: 368 us -> 147 us (0.40)
  waiting for transfers between devices: 293 us -> 0 us
  Pallas kernels: 0 us -> 140 us
  matrix products: 48.3 us -> 0 us
  between operations: 14.9 us -> 1.3 us
  other arithmetic: 10.5 us -> 0 us
    all_gather x1 -> x0, waiting for transfers between devices: 147 us -> none  [on_device(): lax.all_gather(grad_scaled, 'tensor', axis=0, tiled=True)]
    reduce_scatter x1 -> x0, waiting for transfers between devices: 146 us -> none  [on_device(): lax.psum_scatter((running * dequant).astype(jnp.bfloat16), 'dp', scatter_...]
    pallas_call x0 -> x1, Pallas kernels: none -> 140 us  [on_device(): pl.pallas_call(kernel, name='project_grad', out_shape=jax.ShapeDtypeStruc...]
    dot_general x17 -> x0, matrix products: 48.3 us -> none  [the longest x1 27.4 us: on_device(): lax.dot_general(lax.all_gather(grad_scaled, 'tensor', axis=0, tiled=True)...]
    convert_element_type x2 -> x0, other arithmetic: 6.28 us -> none  [the longest x1 3.49 us: quantize(): jnp.clip(values_in * factor, -SATURATION, SATURATION).astype(jnp.bfloat16)]
    reduce_sum x8 -> x0, other arithmetic: 4.19 us -> none  [attend(): jnp.sum(weights, axis=1, keepdims=True)]
  transfers between devices with their start and end apart: 2 -> 0, of which waited for: 2 -> 0; matrix products, arithmetic and copies ran while one was open for 7% -> 0% of each run, Pallas kernels for 0% -> 0%
where the time goes in v1:
time: 147 us; the launch traced here: 145 us
  Pallas kernels  140 us (95%)
  local copies, waits for them, and re-layouts  2.89 us (2%)
    pallas_call x1, Pallas kernels, on_device(): pl.pallas_call(kernel, name='project_grad', out_shape=jax.ShapeDtypeStruc...  140 us

profile of v1, /device:TPU:0, one launch (start us, length us, event | category | flops | bytes accessed | tf_op | source)
XLA Modules:
  0.0 144.6 jit_solution(10103453453170767754)
XLA Ops:
  1.3 140.4 %project_grad.1 = f32[1024,512]{1,0:T(8,128)} custom-call(bf16[1024,1024]{1,0:T(8,128)(2,1)} %q_hbm.1, bf16[1024,128]{1,0:T(8,128)(2,1)} %k_hbm.1, bf16[1024,128]{1,0:T(8,128)(2,1)} %v_hbm.1, bf16[128,8192]{1,0:T(8,128)(2,1)} %g_hbm.1, s32[1]{0:T(128)S(6)} %copy.8.ae_ref, s32[1]{0:T(128)S(6)} %copy.9.ge_ref), custom_call_target="tpu_custom_call" | custom-call | tf_op jit(solution)/shard_map/project_grad/pallas_call | solution.py:331
  141.7 2.9 %copy.7 = f32[512,1024]{1,0:T(8,128)} copy(f32[512,1024]{0,1:T(8,128)} %bitcast.1) | data formatting | bytes 4194304 | tf_op jit(solution)/shard_map/transpose | solution.py:367

commit v2 on v0

v2 whole, which is shorter than its diff:
```python
import math

import jax
import jax.numpy as jnp
from jax import lax
from jax.experimental import pallas as pl
from jax.experimental.pallas import tpu as pltpu
from jax.sharding import PartitionSpec as P

MESH = pl.DeviceIdType.MESH
SATURATION = 448.0
HEAD_DIM = 128
EXPONENT_SCALE = HEAD_DIM**-0.5 * math.log2(math.e)
BF16, F32 = jnp.bfloat16, jnp.float32
VMEM_LIMIT = 67_043_328
OWN, OTHER = 0, 1

STEPS = (
    ("rows", 0), ("rows", 1), ("rows", 2), ("head", 0), ("near", 0), ("head", 1), ("cols", 0), ("rows", 3),
    ("rows", 4), ("head", 2), ("side", 0), ("near", 1), ("head", 3), ("cols", 1), ("rows", 5), ("head", 4),
    ("head", 5), ("cols", 2), ("rows", 6), ("rows", 7), ("pass", 0), ("side", 1), ("near", 2), ("head", 6),
    ("head", 7), ("cols", 3), ("mm", 0, 0, 1), ("mm", 0, 0, 3), ("pass", 1), ("side", 2), ("near", 3),
    ("relay", 0), ("mm", 1, 0, 0), ("mm", 1, 0, 1), ("mm", 1, 0, 3), ("mm", 1, 0, 2), ("mm", 1, 1, 0), ("pass", 2),
    ("side", 3), ("near", 4), ("mm", 0, 1, 0), ("mm", 2, 0, 0), ("mm", 2, 0, 1), ("mm", 2, 0, 2), ("mm", 2, 0, 3),
    ("mm", 2, 1, 0), ("mm", 0, 0, 0), ("pass", 3), ("side", 4), ("near", 5), ("relay", 1), ("mm", 0, 1, 1),
    ("mm", 3, 0, 0), ("mm", 3, 0, 1), ("mm", 3, 0, 2), ("mm", 3, 0, 3), ("mm", 1, 1, 1), ("mm", 3, 1, 0),
    ("pass", 4), ("side", 5), ("near", 6), ("mm", 3, 1, 1), ("mm", 2, 1, 1), ("mm", 4, 0, 1), ("mm", 4, 0, 3),
    ("mm", 4, 1, 0), ("mm", 4, 1, 1), ("mm", 4, 0, 0), ("pass", 5), ("relay", 2), ("mm", 0, 1, 2), ("mm", 1, 1, 2),
    ("side", 6), ("near", 7), ("mm", 3, 1, 2), ("mm", 2, 1, 2), ("mm", 4, 1, 2), ("mm", 5, 0, 0), ("mm", 5, 0, 1),
    ("mm", 5, 0, 3), ("mm", 5, 1, 0), ("mm", 5, 1, 1), ("mm", 5, 1, 2), ("mm", 0, 0, 2), ("pass", 6), ("side", 7),
    ("mm", 4, 0, 2), ("mm", 6, 1, 1), ("mm", 6, 0, 1), ("mm", 6, 0, 3), ("mm", 6, 0, 0), ("mm", 6, 0, 2),
    ("mm", 6, 1, 0), ("mm", 6, 1, 2), ("pass", 7), ("relay", 3), ("mm", 0, 1, 3), ("mm", 1, 1, 3), ("mm", 2, 1, 3),
    ("mm", 5, 1, 3), ("mm", 7, 0, 1), ("mm", 7, 1, 1), ("mm", 7, 0, 3), ("mm", 4, 1, 3), ("mm", 3, 1, 3),
    ("mm", 7, 1, 0), ("mm", 5, 0, 2), ("mm", 7, 1, 2), ("mm", 6, 1, 3), ("mm", 7, 1, 3), ("mm", 7, 0, 0),
    ("mm", 7, 0, 2),
)
BLOCKS = ((0, 1), (0, 0), (2, 0), (1, 0), (1, 1), (2, 1), (3, 0), (3, 1))
EARLY = (0, 2)
WAY = ((0, 0, 1, 1), (0, 1, 1, 0))
SHIFT = (2, 1, 3, 0)


def kernel(q_hbm, k_hbm, v_hbm, g_hbm, ae_ref, ge_ref, out_ref,
           q_ref, k_ref, v_ref, g_in, vt_ref, g_send, g_all, at_own, at_oth,
           z2_send, z2_recv, zf_send, zf_recv, f_send, f_recv, p_send, p_recv, e_send, e_recv, s_send, s_recv,
           in_sem, s1_ssem, s1_rsem, x_ssem, x_rsem, xf_ssem, xf_rsem, a_ssem, a_rsem,
           z2_ssem, z2_rsem, zf_ssem, zf_rsem, f_ssem, f_rsem, l_ssem, l_rsem):
    d = lax.axis_index("dp")
    t = lax.axis_index("tensor")
    yh, z, c = lax.div(d, 8), lax.rem(lax.div(d, 2), 4), lax.rem(d, 2)
    low, x = lax.div(t, 4), lax.rem(t, 4)
    half = lax.rem(low + yh, 2)
    partner_dp = d + 1 - 2 * c
    side_t = (1 - low) * 4 + x
    x_up, x_down, x_far = lax.rem(x + 1, 4), lax.rem(x + 3, 4), lax.rem(x + 2, 4)
    z_up, z_down = lax.rem(z + 1, 4), lax.rem(z + 3, 4)

    def dev(dp, tensor):
        return {"dp": dp, "tensor": tensor}

    core_dev, side_dev, cross_dev = dev(partner_dp, t), dev(d, side_t), dev(partner_dp, side_t)
    x_devs = dev(d, low * 4 + x_up), dev(d, low * 4 + x_down)
    z_devs = dev(yh * 8 + z_up * 2 + c, t), dev(yh * 8 + z_down * 2 + c, t)
    far_dev = dev((1 - yh) * 8 + z * 2 + c, side_t)
    quarter_dev = (core_dev, side_dev, cross_dev)
    quarter_slot = ((1 - c, low), (c, 1 - low), (1 - c, 1 - low))

    sends = []

    def remote(src, dst, ssem, rsem, to):
        return pltpu.make_async_remote_copy(
            src_ref=src, dst_ref=dst, send_sem=ssem, recv_sem=rsem, device_id=to, device_id_type=MESH
        )

    def start(copy):
        copy.start()
        sends.append(copy)

    loads = [
        pltpu.make_async_copy(src, dst, in_sem.at[i])
        for i, (src, dst) in enumerate(((g_hbm, g_in), (k_hbm, k_ref), (v_hbm, v_ref), (q_hbm, q_ref)))
    ]
    for load in loads:
        load.start()
    barrier = pltpu.get_barrier_semaphore()
    for to in (core_dev, side_dev, cross_dev, *x_devs, *z_devs, far_dev):
        pl.semaphore_signal(barrier, inc=1, device_id=to, device_id_type=MESH)

    grad_factor = SATURATION * jnp.exp2(jnp.full((1, 256), -ge_ref[0], jnp.int32).astype(F32))
    act_factor = SATURATION * jnp.exp2(jnp.full((1, 256), -ae_ref[0], jnp.int32).astype(F32))
    dequant = jnp.exp2(jnp.full((1, 256), ae_ref[0] + ge_ref[0], jnp.int32).astype(F32)) / (
        SATURATION * SATURATION
    )

    loads[0].wait()

    def scaled(block):
        values = g_in[:, pl.ds(pl.multiple_of(block * 256, 256), 256)].astype(F32)
        return jnp.clip(values * grad_factor, -SATURATION, SATURATION).astype(BF16)

    for o, (role, near) in enumerate(BLOCKS):
        to_yh = yh if near else 1 - yh
        base = to_yh * 16 + lax.rem(z + SHIFT[role], 4) * 4
        g_send[1, o] = scaled(base + 2 * c + 1 - half)
        g_send[2, o] = scaled(base + 2 * (1 - c) + 1 - half)
        g_send[0, o] = scaled(base + 2 * (1 - c) + half)
        g_all[o, c, low, x] = scaled(base + 2 * c + half)
    pl.semaphore_wait(barrier, 8)

    def s1_send(k, o):
        start(remote(g_send.at[k, o], g_all.at[o, c, low, x], s1_ssem.at[k, o], s1_rsem.at[k, o], quarter_dev[k]))

    def s1_wait(k, o):
        s, l = quarter_slot[k]
        remote(g_send.at[k, o], g_all.at[o, s, l, x], s1_ssem.at[k, o], s1_rsem.at[k, o], quarter_dev[k]).wait_recv()

    def x_copy(o, i, part, at):
        ref = g_all.at[o, :, 1 - low if part else low, at]
        return remote(ref, ref, x_ssem.at[i, part, o], x_rsem.at[i, part, o], x_devs[i])

    def xf_copy(o, i, at):
        ref = g_all.at[o, i, :, at]
        return remote(ref, ref, xf_ssem.at[i, o], xf_rsem.at[i, o], x_devs[i])

    def a_copy(i, q):
        rows = pl.ds(q * 256, 256)
        src = (at_oth if i == 2 else at_own).at[c, rows]
        dst = (at_own if i == 0 else at_oth).at[c, rows]
        return remote(src, dst, a_ssem.at[i, q], a_rsem.at[i, q], (core_dev, side_dev, core_dev)[i])

    def a_wait(i, q):
        rows = pl.ds(q * 256, 256)
        ref = (at_own if i == 0 else at_oth).at[c if i == 1 else 1 - c, rows]
        remote(ref, ref, a_ssem.at[i, q], a_rsem.at[i, q], (core_dev, side_dev, core_dev)[i]).wait_recv()

    have = set()

    def need(key, wait):
        if key not in have:
            have.add(key)
            wait()

    def need_x(o, i, part):
        need(("x", o, i, part), lambda: x_copy(o, i, part, (x_down, x_up)[i]).wait_recv())

    def head(index):
        columns = slice(index * HEAD_DIM, (index + 1) * HEAD_DIM)
        for tb in range(4):
            rows = slice(tb * 256, (tb + 1) * 256)
            query = q_ref[rows, columns]

            def scores_of(keys):
                return lax.dot_general(keys, query, (((1,), (1,)), ((), ())), preferred_element_type=F32)

            last = jnp.where(causal, scores_of(k_ref[rows, :]), F32(-1e30))
            top = jnp.max(last, axis=0, keepdims=True)
            if tb > 0:
                early = scores_of(k_ref[: tb * 256, :])
                top = jnp.maximum(top, jnp.max(early, axis=0, keepdims=True))
            weights = jnp.exp2((last - top) * EXPONENT_SCALE)
            total = jnp.sum(weights, axis=0, keepdims=True)
            value = jnp.dot(vt_ref[:, rows], weights.astype(BF16), preferred_element_type=F32)
            if tb > 0:
                weights = jnp.exp2((early - top) * EXPONENT_SCALE)
                total += jnp.sum(weights, axis=0, keepdims=True)
                value += jnp.dot(vt_ref[:, : tb * 256], weights.astype(BF16), preferred_element_type=F32)
            value = jnp.clip(value * (act_factor / total), -SATURATION, SATURATION).astype(BF16)
            at_own[c, columns, rows] = value

    def z2_copy(stream, which, q):
        way = WAY[which][q]
        return remote(z2_send.at[stream, q], z2_recv.at[stream, q], z2_ssem.at[stream, q], z2_rsem.at[stream, q],
                      z_devs[way])

    def zf_copy(way, stream, q):
        return remote(zf_send.at[way, stream, q], zf_recv.at[way, stream, q], zf_ssem.at[way, stream, q],
                      zf_rsem.at[way, stream, q], z_devs[way])

    def f_copy(role, to_which, q):
        at = role, to_which, EARLY.index(q)
        return remote(f_send.at[at], f_recv.at[at], f_ssem.at[at], f_rsem.at[at], far_dev)

    def last_copy(i, q):
        send, recv = (p_send, e_send, s_send)[i], (p_recv, e_recv, s_recv)[i]
        return remote(send.at[q], recv.at[q], l_ssem.at[i, q], l_rsem.at[i, q], (far_dev, far_dev, side_dev)[i])

    def multiply(o, which, q):
        role, near = BLOCKS[o]
        stream = 2 * near + which
        early = q in EARLY
        for part in range(2):
            need(("s1", o, part), None)
            for i in range(2):
                need_x(o, i, part)
        for i in range(2):
            need(("xf", o, i), lambda: xf_copy(o, i, x_far).wait_recv())
        if which == OWN:
            need(("a0", q), lambda: a_wait(0, q))
        else:
            need(("a1", q), None)
            need(("a2", q), lambda: a_wait(2, q))
        adds, copy, dst = [], None, None
        if early and not near:
            copy = f_copy(role, 1 - which, q)
            dst = f_send.at[role, 1 - which, EARLY.index(q)]
        else:
            if early:
                f_copy(role, which, q).wait_recv()
                adds.append(f_recv.at[role, which, EARLY.index(q)])
            if role == 0:
                dst, copy = z2_send.at[stream, q], z2_copy(stream, which, q)
            elif role < 3:
                way = role - 1
                dst, copy = zf_send.at[way, stream, q], zf_copy(way, stream, q)
                if way == WAY[which][q]:
                    z2_copy(stream, which, q).wait_recv()
                    adds.append(z2_recv.at[stream, q])
            else:
                for way in range(2):
                    zf_copy(way, stream, q).wait_recv()
                    adds.append(zf_recv.at[way, stream, q])
                if not near:
                    dst, copy = ((p_send, e_send)[which].at[q], last_copy(which, q))
                elif which == OTHER:
                    dst, copy = s_send.at[q], last_copy(2, q)
                    if not early:
                        last_copy(0, q).wait_recv()
                        adds.append(p_recv.at[q])
        at = (at_own, at_oth)[which]
        rows = slice(q * 256, (q + 1) * 256)
        total = jnp.dot(at[0, rows, :], g_all[o, 0].reshape(1024, 256), preferred_element_type=F32)
        total += jnp.dot(at[1, rows, :], g_all[o, 1].reshape(1024, 256), preferred_element_type=F32)
        for add in adds:
            total += add[...].astype(F32)
        if copy is None:
            out_ref[rows, pl.ds(pl.multiple_of(half * 256, 256), 256)] = total * dequant
        else:
            dst[...] = total.astype(BF16)
            start(copy)

    for o in range(8):
        s1_send(0, o)
    causal = None
    for step in STEPS:
        kind, at = step[0], step[1]
        if kind == "rows":
            s1_send(1, at)
            s1_send(2, at)
        elif kind == "near":
            s1_wait(0, at)
            have.add(("s1", at, 0))
            for i in range(2):
                start(x_copy(at, i, 0, x))
        elif kind == "side":
            s1_wait(1, at)
            s1_wait(2, at)
            have.add(("s1", at, 1))
            for i in range(2):
                start(x_copy(at, i, 1, x))
        elif kind == "pass":
            for i in range(2):
                need_x(at, i, 0)
                need_x(at, i, 1)
                start(xf_copy(at, i, (x_down, x_up)[i]))
        elif kind == "head":
            if at == 0:
                for load in loads[1:]:
                    load.wait()
                vt_ref[...] = v_ref[...].astype(F32).T.astype(BF16)
                causal = lax.broadcasted_iota(jnp.int32, (256, 256), 0) <= lax.broadcasted_iota(
                    jnp.int32, (256, 256), 1
                )
            head(at)
        elif kind == "cols":
            start(a_copy(0, at))
            start(a_copy(1, at))
        elif kind == "relay":
            a_wait(1, at)
            have.add(("a1", at))
            start(a_copy(2, at))
        else:
            multiply(*step[1:])

    for q in range(4):
        rows = slice(q * 256, (q + 1) * 256)
        if q not in EARLY:
            last_copy(1, q).wait_recv()
            out_ref[rows, pl.ds(pl.multiple_of(half * 256, 256), 256)] += e_recv[q].astype(F32) * dequant
    for q in range(4):
        rows = slice(q * 256, (q + 1) * 256)
        last_copy(2, q).wait_recv()
        out_ref[rows, pl.ds(pl.multiple_of((1 - half) * 256, 256), 256)] = s_recv[q].astype(F32) * dequant
    for copy in sends:
        copy.wait_send()


def on_device(queries, keys, values, out_grad, act_exponent, grad_exponent):
    anywhere = pl.BlockSpec(memory_space=pl.ANY)
    scalar = pl.BlockSpec(memory_space=pltpu.SMEM)
    dma = pltpu.SemaphoreType.DMA
    early = max(len(EARLY), 1)
    tile = (256, 256)
    transposed = pl.pallas_call(
        kernel,
        name="project_grad",
        out_shape=jax.ShapeDtypeStruct((1024, 512), F32),
        in_specs=[anywhere] * 4 + [scalar] * 2,
        out_specs=pl.BlockSpec(memory_space=pltpu.VMEM),
        scratch_shapes=[
            pltpu.VMEM((1024, 1024), BF16),
            pltpu.VMEM((1024, 128), BF16),
            pltpu.VMEM((1024, 128), BF16),
            pltpu.VMEM((128, 8192), BF16),
            pltpu.VMEM((128, 1024), BF16),
            pltpu.VMEM((3, 8, 128, 256), BF16),
            pltpu.VMEM((8, 2, 2, 4, 128, 256), BF16),
            pltpu.VMEM((2, 1024, 1024), BF16),
            pltpu.VMEM((2, 1024, 1024), BF16),
            pltpu.VMEM((4, 4, *tile), BF16), pltpu.VMEM((4, 4, *tile), BF16),
            pltpu.VMEM((2, 4, 4, *tile), BF16), pltpu.VMEM((2, 4, 4, *tile), BF16),
            pltpu.VMEM((4, 2, early, *tile), BF16), pltpu.VMEM((4, 2, early, *tile), BF16),
            pltpu.VMEM((4, *tile), BF16), pltpu.VMEM((4, *tile), BF16),
            pltpu.VMEM((4, *tile), BF16), pltpu.VMEM((4, *tile), BF16),
            pltpu.VMEM((4, *tile), BF16), pltpu.VMEM((4, *tile), BF16),
            dma((4,)),
            dma((3, 8)), dma((3, 8)),
            dma((2, 2, 8)), dma((2, 2, 8)),
            dma((2, 8)), dma((2, 8)),
            dma((3, 4)), dma((3, 4)),
            dma((4, 4)), dma((4, 4)),
            dma((2, 4, 4)), dma((2, 4, 4)),
            dma((4, 2, early)), dma((4, 2, early)),
            dma((3, 4)), dma((3, 4)),
        ],
        compiler_params=pltpu.CompilerParams(
            collective_id=0, has_side_effects=True, vmem_limit_bytes=VMEM_LIMIT
        ),
    )(queries, keys, values, out_grad, act_exponent, grad_exponent)
    return transposed.T


def solution(mesh):
    in_specs = (
        P("dp", "tensor"),
        P("dp", "tensor"),
        P("dp", "tensor"),
        P(("dp", "tensor"), None),
        P(),
        P(),
    )
    return jax.shard_map(
        on_device, mesh=mesh, in_specs=in_specs, out_specs=P("dp", "tensor"), check_vma=False
    )
```

time: 368 us -> 115 us (0.31)
  waiting for transfers between devices: 293 us -> 0 us
  Pallas kernels: 0 us -> 111 us
  matrix products: 48.3 us -> 0 us
  between operations: 14.9 us -> 1.31 us
  other arithmetic: 10.5 us -> 0 us
    all_gather x1 -> x0, waiting for transfers between devices: 147 us -> none  [on_device(): lax.all_gather(grad_scaled, 'tensor', axis=0, tiled=True)]
    reduce_scatter x1 -> x0, waiting for transfers between devices: 146 us -> none  [on_device(): lax.psum_scatter((running * dequant).astype(jnp.bfloat16), 'dp', scatter_...]
    pallas_call x0 -> x1, Pallas kernels: none -> 111 us  [on_device(): pl.pallas_call(kernel, name='project_grad', out_shape=jax.ShapeDtypeStruc...]
    dot_general x17 -> x0, matrix products: 48.3 us -> none  [the longest x1 27.4 us: on_device(): lax.dot_general(lax.all_gather(grad_scaled, 'tensor', axis=0, tiled=True)...]
    convert_element_type x2 -> x0, other arithmetic: 6.28 us -> none  [the longest x1 3.49 us: quantize(): jnp.clip(values_in * factor, -SATURATION, SATURATION).astype(jnp.bfloat16)]
    reduce_sum x8 -> x0, other arithmetic: 4.19 us -> none  [attend(): jnp.sum(weights, axis=1, keepdims=True)]
  transfers between devices with their start and end apart: 2 -> 0, of which waited for: 2 -> 0; matrix products, arithmetic and copies ran while one was open for 7% -> 0% of each run, Pallas kernels for 0% -> 0%
where the time goes in v2:
time: 115 us
  Pallas kernels  111 us (97%)
  local copies, waits for them, and re-layouts  2.89 us (3%)
  between operations  1.31 us (1%)
    pallas_call x1, Pallas kernels, on_device(): pl.pallas_call(kernel, name='project_grad', out_shape=jax.ShapeDtypeStruc...  111 us
    transpose x1, local copies, waits for them, and re-layouts, on_device(): return transposed.T  2.89 us

profile of v2, /device:TPU:0, one launch (start us, length us, event | category | flops | bytes accessed | tf_op | source)
XLA Modules:
  0.0 115.0 jit_solution(15169024445031688746)
XLA Ops:
  1.3 110.8 %project_grad.1 = f32[1024,512]{1,0:T(8,128)} custom-call(bf16[1024,1024]{1,0:T(8,128)(2,1)} %q_hbm.1, bf16[1024,128]{1,0:T(8,128)(2,1)} %k_hbm.1, bf16[1024,128]{1,0:T(8,128)(2,1)} %v_hbm.1, bf16[128,8192]{1,0:T(8,128)(2,1)} %g_hbm.1, s32[1]{0:T(128)S(6)} %copy.8.ae_ref, s32[1]{0:T(128)S(6)} %copy.9.ge_ref), custom_call_target="tpu_custom_call" | custom-call | tf_op jit(solution)/shard_map/project_grad/pallas_call | solution.py:303
  112.1 2.9 %copy.7 = f32[512,1024]{1,0:T(8,128)} copy(f32[512,1024]{0,1:T(8,128)} %bitcast.1) | data formatting | bytes 4194304 | tf_op jit(solution)/shard_map/transpose | solution.py:339

commit v3 on v2

v3 whole, which is shorter than its diff:
```python
import math

import jax
import jax.numpy as jnp
from jax import lax
from jax.experimental import pallas as pl
from jax.experimental.pallas import tpu as pltpu
from jax.sharding import PartitionSpec as P

MESH = pl.DeviceIdType.MESH
SATURATION = 448.0
HEAD_DIM = 128
EXPONENT_SCALE = HEAD_DIM**-0.5 * math.log2(math.e)
BF16, F32 = jnp.bfloat16, jnp.float32
VMEM_LIMIT = 67_043_328
OWN, OTHER = 0, 1

STEPS = (
    ("rows", 0), ("rows", 1), ("rows", 2), ("self", 0), ("self", 1), ("head", 0), ("near", 0), ("head", 1),
    ("cols", 0), ("rows", 3), ("rows", 4), ("rows", 5), ("head", 2), ("head", 3), ("cols", 1), ("side", 0),
    ("near", 1), ("head", 4), ("head", 5), ("cols", 2), ("rows", 6), ("rows", 7), ("head", 6), ("pass", 0),
    ("side", 1), ("self", 2), ("near", 2), ("head", 7), ("cols", 3), ("mm", 0, 0, 1), ("mm", 0, 0, 0), ("pass", 1),
    ("side", 2), ("self", 3), ("near", 3), ("relay", 0), ("mm", 1, 0, 1), ("pass", 2), ("side", 3), ("self", 4),
    ("near", 4), ("mm", 2, 0, 1), ("mm", 2, 0, 0), ("pass", 3), ("side", 4), ("self", 5), ("near", 5),
    ("mm", 3, 0, 1), ("relay", 1), ("pass", 4), ("side", 5), ("self", 6), ("near", 6), ("mm", 2, 1, 0),
    ("mm", 1, 1, 0), ("mm", 3, 1, 0), ("mm", 0, 1, 0), ("mm", 4, 0, 1), ("mm", 4, 0, 0), ("mm", 4, 1, 0),
    ("pass", 5), ("relay", 2), ("mm", 3, 0, 0), ("mm", 4, 1, 1), ("mm", 0, 1, 1), ("side", 6), ("self", 7),
    ("near", 7), ("mm", 1, 1, 1), ("mm", 5, 0, 1), ("mm", 5, 1, 1), ("mm", 1, 0, 0), ("pass", 6), ("side", 7),
    ("mm", 2, 1, 1), ("mm", 5, 1, 0), ("mm", 3, 1, 1), ("mm", 6, 0, 0), ("mm", 6, 0, 1), ("mm", 6, 1, 0),
    ("pass", 7), ("relay", 3), ("mm", 6, 1, 1), ("mm", 0, 1, 2), ("mm", 1, 1, 2), ("mm", 4, 1, 2), ("mm", 5, 1, 2),
    ("mm", 7, 0, 1), ("mm", 5, 0, 0), ("mm", 2, 1, 2), ("mm", 7, 1, 1), ("mm", 3, 1, 2), ("mm", 7, 1, 0),
    ("mm", 6, 1, 2), ("mm", 7, 1, 2), ("mm", 7, 0, 0),
)
BLOCKS = ((0, 0), (0, 1), (1, 0), (1, 1), (2, 0), (2, 1), (3, 0), (3, 1))
EARLY = (0, 1)
WAY = ((1, 0), (1, 0, 0))
SHIFT = (2, 1, 3, 0)
GROUPS = ((0, 1), (2, 3)), ((0, 1), (2,), (3,))


def kernel(q_hbm, k_hbm, v_hbm, g_hbm, ae_ref, ge_ref, out_ref,
           q_ref, k_ref, v_ref, g_in, vt_ref, g_send, g_all, at_own, at_oth,
           z2_send, z2_recv, zf_send, zf_recv, f_send, f_recv, p_send, p_recv, e_send, e_recv, s_send, s_recv, out_v,
           in_sem, s1_ssem, s1_rsem, x_ssem, x_rsem, xf_ssem, xf_rsem, a_ssem, a_rsem,
           z2_ssem, z2_rsem, zf_ssem, zf_rsem, f_ssem, f_rsem, l_ssem, l_rsem, out_sem):
    d = lax.axis_index("dp")
    t = lax.axis_index("tensor")
    yh, z, c = lax.div(d, 8), lax.rem(lax.div(d, 2), 4), lax.rem(d, 2)
    low, x = lax.div(t, 4), lax.rem(t, 4)
    half = lax.rem(low + yh, 2)
    partner_dp = d + 1 - 2 * c
    side_t = (1 - low) * 4 + x
    x_up, x_down, x_far = lax.rem(x + 1, 4), lax.rem(x + 3, 4), lax.rem(x + 2, 4)
    z_up, z_down = lax.rem(z + 1, 4), lax.rem(z + 3, 4)

    def dev(dp, tensor):
        return {"dp": dp, "tensor": tensor}

    core_dev, side_dev, cross_dev = dev(partner_dp, t), dev(d, side_t), dev(partner_dp, side_t)
    x_devs = dev(d, low * 4 + x_up), dev(d, low * 4 + x_down)
    z_devs = dev(yh * 8 + z_up * 2 + c, t), dev(yh * 8 + z_down * 2 + c, t)
    far_dev = dev((1 - yh) * 8 + z * 2 + c, side_t)
    quarter_dev = (core_dev, side_dev, cross_dev)
    quarter_slot = ((1 - c, low), (c, 1 - low), (1 - c, 1 - low))

    def remote(src, dst, ssem, rsem, to):
        return pltpu.make_async_remote_copy(
            src_ref=src, dst_ref=dst, send_sem=ssem, recv_sem=rsem, device_id=to, device_id_type=MESH
        )

    def start(make, *key):
        make(*key).start()

    def sent(ref, ssem):
        remote(ref, ref, ssem, in_sem.at[0], core_dev).wait_send()

    loads = [
        pltpu.make_async_copy(src, dst, in_sem.at[i])
        for i, (src, dst) in enumerate(((g_hbm, g_in), (k_hbm, k_ref), (v_hbm, v_ref), (q_hbm, q_ref)))
    ]
    for load in loads:
        load.start()
    barrier = pltpu.get_barrier_semaphore()
    for to in (core_dev, side_dev, cross_dev, *x_devs, *z_devs, far_dev):
        pl.semaphore_signal(barrier, inc=1, device_id=to, device_id_type=MESH)

    grad_factor = SATURATION * jnp.exp2(jnp.full((1, 256), -ge_ref[0], jnp.int32).astype(F32))
    act_factor = SATURATION * jnp.exp2(jnp.full((1, 256), -ae_ref[0], jnp.int32).astype(F32))
    dequant = jnp.exp2(jnp.full((1, 256), ae_ref[0] + ge_ref[0], jnp.int32).astype(F32)) / (
        SATURATION * SATURATION
    )

    loads[0].wait()

    def scaled(block):
        values = g_in[:, pl.ds(pl.multiple_of(block * 256, 256), 256)].astype(F32)
        return jnp.clip(values * grad_factor, -SATURATION, SATURATION).astype(BF16)

    for o, (role, near) in enumerate(BLOCKS):
        to_yh = yh if near else 1 - yh
        base = to_yh * 16 + lax.rem(z + SHIFT[role], 4) * 4
        g_send[1, o] = scaled(base + 2 * c + 1 - half)
        g_send[2, o] = scaled(base + 2 * (1 - c) + 1 - half)
        g_send[0, o] = scaled(base + 2 * (1 - c) + half)
        g_all[o, c, low, x] = scaled(base + 2 * c + half)
    pl.semaphore_wait(barrier, 8)

    def s1_copy(k, o):
        return remote(g_send.at[k, o], g_all.at[o, c, low, x], s1_ssem.at[0], s1_rsem.at[k, o], quarter_dev[k])

    def s1_wait(k, o):
        s, l = quarter_slot[k]
        remote(g_send.at[k, o], g_all.at[o, s, l, x], s1_ssem.at[0], s1_rsem.at[k, o], quarter_dev[k]).wait_recv()

    def x_copy(o, i, part, at):
        if part == 2:
            ref = g_all.at[o, :, 1 - low, at]
        else:
            ref = g_all.at[o, 1 - c if part else c, low, at]
        return remote(ref, ref, x_ssem.at[i], x_rsem.at[i, o], x_devs[i])

    def xf_copy(o, i, at):
        ref = g_all.at[o, i, :, at]
        return remote(ref, ref, xf_ssem.at[i], xf_rsem.at[i, o], x_devs[i])

    def a_copy(i, q):
        rows = pl.ds(q * 256, 256)
        src = (at_oth if i == 2 else at_own).at[c, rows]
        dst = (at_own if i == 0 else at_oth).at[c, rows]
        return remote(src, dst, a_ssem.at[i], a_rsem.at[i, q], (core_dev, side_dev, core_dev)[i])

    def a_wait(i, q):
        rows = pl.ds(q * 256, 256)
        ref = (at_own if i == 0 else at_oth).at[c if i == 1 else 1 - c, rows]
        remote(ref, ref, a_ssem.at[i], a_rsem.at[i, q], (core_dev, side_dev, core_dev)[i]).wait_recv()

    have = set()

    def need(key, wait):
        if key not in have:
            have.add(key)
            wait()

    def need_x(o, i):
        ref = g_all.at[o, :, :, (x_down, x_up)[i]]
        need(("x", o, i), lambda: remote(ref, ref, x_ssem.at[i], x_rsem.at[i, o], x_devs[i]).wait_recv())

    def head(index):
        columns = slice(index * HEAD_DIM, (index + 1) * HEAD_DIM)
        for tb in range(4):
            rows = slice(tb * 256, (tb + 1) * 256)
            query = q_ref[rows, columns]

            def scores_of(keys):
                return lax.dot_general(keys, query, (((1,), (1,)), ((), ())), preferred_element_type=F32)

            last = jnp.where(causal, scores_of(k_ref[rows, :]), F32(-1e30))
            top = jnp.max(last, axis=0, keepdims=True)
            if tb > 0:
                early = scores_of(k_ref[: tb * 256, :])
                top = jnp.maximum(top, jnp.max(early, axis=0, keepdims=True))
            weights = jnp.exp2((last - top) * EXPONENT_SCALE)
            total = jnp.sum(weights, axis=0, keepdims=True)
            value = jnp.dot(vt_ref[:, rows], weights.astype(BF16), preferred_element_type=F32)
            if tb > 0:
                weights = jnp.exp2((early - top) * EXPONENT_SCALE)
                total += jnp.sum(weights, axis=0, keepdims=True)
                value += jnp.dot(vt_ref[:, : tb * 256], weights.astype(BF16), preferred_element_type=F32)
            value = jnp.clip(value * (act_factor / total), -SATURATION, SATURATION).astype(BF16)
            at_own[c, columns, rows] = value

    def z2_copy(stream, way, q):
        return remote(z2_send.at[stream, q], z2_recv.at[stream, q], z2_ssem.at[stream // 2], z2_rsem.at[stream, q],
                      z_devs[way])

    def zf_copy(way, stream, q):
        return remote(zf_send.at[way, stream, q], zf_recv.at[way, stream, q], zf_ssem.at[stream // 2],
                      zf_rsem.at[way, stream, q], z_devs[way])

    def f_copy(role, to_which, q):
        at = role, to_which, q - EARLY[0]
        return remote(f_send.at[at], f_recv.at[at], f_ssem.at[0], f_rsem.at[at], far_dev)

    def last_copy(i, q):
        send, recv = (p_send, e_send, s_send)[i], (p_recv, e_recv, s_recv)[i]
        return remote(send.at[q], recv.at[q], l_ssem.at[i], l_rsem.at[i, q], (far_dev, far_dev, side_dev)[i])

    def out_copy(part, q):
        side = 1 - half if part else half
        to = out_ref.at[pl.ds(q * 256, 256), pl.ds(pl.multiple_of(side * 256, 256), 256)]
        return pltpu.make_async_copy(out_v.at[part, q], to, out_sem.at[part, q])

    def multiply(o, which, group):
        role, near = BLOCKS[o]
        quarters = GROUPS[which][group]
        stream, way2 = 2 * near + which, WAY[which][group]
        early = quarters[0] in EARLY
        for part in range(3):
            need(("s1", o, part), None)
        for i in range(2):
            need_x(o, i)
            need(("xf", o, i), lambda: xf_copy(o, i, x_far).wait_recv())
        adds, make, key, send = [], None, (), None
        for q in quarters:
            need(("cols", q) if which == OWN else ("relay", q), None)
            need(("a", which, q), lambda: a_wait(2 * which, q))
        if early and not near:
            make, key, send = f_copy, (role, 1 - which), lambda q: f_send.at[role, 1 - which, q - EARLY[0]]
        else:
            if early:
                for q in quarters:
                    f_copy(role, which, q).wait_recv()
                adds.append(lambda q: f_recv.at[role, which, q - EARLY[0]])
            if role == 0:
                make, key, send = z2_copy, (stream, way2), lambda q: z2_send.at[stream, q]
            elif role < 3:
                make, key, send = zf_copy, (role - 1, stream), lambda q: zf_send.at[role - 1, stream, q]
                if role - 1 == way2:
                    for q in quarters:
                        z2_copy(stream, way2, q).wait_recv()
                    adds.append(lambda q: z2_recv.at[stream, q])
            else:
                for q in quarters:
                    for way in range(2):
                        zf_copy(way, stream, q).wait_recv()
                adds += [lambda q: zf_recv.at[0, stream, q], lambda q: zf_recv.at[1, stream, q]]
                if not near:
                    make, key, send = last_copy, (which,), lambda q: (p_send, e_send)[which].at[q]
                elif which == OTHER:
                    make, key, send = last_copy, (2,), lambda q: s_send.at[q]
                    if not early:
                        for q in quarters:
                            last_copy(0, q).wait_recv()
                        adds.append(lambda q: p_recv.at[q])
        at = (at_own, at_oth)[which]

        def tile(q):
            rows = pl.ds(q * 256 if isinstance(q, int) else pl.multiple_of(q * 256, 256), 256)
            total = jnp.dot(at[0, rows, :], g_all[o, 0].reshape(1024, 256), preferred_element_type=F32)
            total += jnp.dot(at[1, rows, :], g_all[o, 1].reshape(1024, 256), preferred_element_type=F32)
            for add in adds:
                total += add(q)[...].astype(F32)
            if make is None:
                out_v[0, q] = total * dequant
                if early:
                    out_copy(0, q).start()
            else:
                send(q)[...] = total.astype(BF16)
                make(*key, q).start()

        if len(quarters) == 1:
            tile(quarters[0])
        else:
            lax.fori_loop(0, len(quarters), lambda i, carry: (tile(quarters[0] + i), carry)[1], 0)

    for o in range(8):
        start(s1_copy, 0, o)
    causal = None
    for step in STEPS:
        kind, at = step[0], step[1]
        if kind == "rows":
            start(s1_copy, 1, at)
            start(s1_copy, 2, at)
        elif kind == "self":
            have.add(("s1", at, 0))
            for i in range(2):
                start(x_copy, at, i, 0, x)
        elif kind == "near":
            s1_wait(0, at)
            have.add(("s1", at, 1))
            for i in range(2):
                start(x_copy, at, i, 1, x)
        elif kind == "side":
            s1_wait(1, at)
            s1_wait(2, at)
            have.add(("s1", at, 2))
            for i in range(2):
                start(x_copy, at, i, 2, x)
        elif kind == "pass":
            for i in range(2):
                need_x(at, i)
                start(xf_copy, at, i, (x_down, x_up)[i])
        elif kind == "head":
            if at == 0:
                for load in loads[1:]:
                    load.wait()
                vt_ref[...] = v_ref[...].astype(F32).T.astype(BF16)
                causal = lax.broadcasted_iota(jnp.int32, (256, 256), 0) <= lax.broadcasted_iota(
                    jnp.int32, (256, 256), 1
                )
            head(at)
        elif kind == "cols":
            have.add(("cols", at))
            start(a_copy, 0, at)
            start(a_copy, 1, at)
        elif kind == "relay":
            a_wait(1, at)
            have.add(("relay", at))
            start(a_copy, 2, at)
        else:
            multiply(*step[1:])

    for q in range(4):
        if q not in EARLY:
            last_copy(1, q).wait_recv()
            out_v[0, q] += e_recv[q].astype(F32) * dequant
            out_copy(0, q).start()
    for q in range(4):
        last_copy(2, q).wait_recv()
        out_v[1, q] = s_recv[q].astype(F32) * dequant
        out_copy(1, q).start()
    late = slice(0, 4)
    if EARLY:
        late = slice(2, 4) if EARLY[0] == 0 else slice(0, 2)
        sent(f_send, f_ssem.at[0])
    sent(g_send, s1_ssem.at[0])
    for i in range(2):
        sent(g_all.at[:, :, :, x], x_ssem.at[i])
        sent(g_all.at[:, i, :, (x_down, x_up)[i]], xf_ssem.at[i])
        sent((p_send, e_send)[i].at[late], l_ssem.at[i])
    for i, ref in enumerate((at_own, at_own, at_oth)):
        sent(ref.at[c], a_ssem.at[i])
    sent(z2_send.at[2:4], z2_ssem.at[1])
    sent(z2_send.at[0:2, late], z2_ssem.at[0])
    sent(zf_send.at[:, 2:4], zf_ssem.at[1])
    sent(zf_send.at[:, 0:2, late], zf_ssem.at[0])
    sent(s_send, l_ssem.at[2])
    for q in range(4):
        for part in range(2):
            out_copy(part, q).wait()


def on_device(queries, keys, values, out_grad, act_exponent, grad_exponent):
    anywhere = pl.BlockSpec(memory_space=pl.ANY)
    scalar = pl.BlockSpec(memory_space=pltpu.SMEM)
    dma = pltpu.SemaphoreType.DMA
    early = max(len(EARLY), 1)
    tile = (256, 256)
    transposed = pl.pallas_call(
        kernel,
        name="project_grad",
        out_shape=jax.ShapeDtypeStruct((1024, 512), F32),
        in_specs=[anywhere] * 4 + [scalar] * 2,
        out_specs=anywhere,
        scratch_shapes=[
            pltpu.VMEM((1024, 1024), BF16),
            pltpu.VMEM((1024, 128), BF16),
            pltpu.VMEM((1024, 128), BF16),
            pltpu.VMEM((128, 8192), BF16),
            pltpu.VMEM((128, 1024), BF16),
            pltpu.VMEM((3, 8, 128, 256), BF16),
            pltpu.VMEM((8, 2, 2, 4, 128, 256), BF16),
            pltpu.VMEM((2, 1024, 1024), BF16),
            pltpu.VMEM((2, 1024, 1024), BF16),
            pltpu.VMEM((4, 4, *tile), BF16), pltpu.VMEM((4, 4, *tile), BF16),
            pltpu.VMEM((2, 4, 4, *tile), BF16), pltpu.VMEM((2, 4, 4, *tile), BF16),
            pltpu.VMEM((4, 2, early, *tile), BF16), pltpu.VMEM((4, 2, early, *tile), BF16),
            pltpu.VMEM((4, *tile), BF16), pltpu.VMEM((4, *tile), BF16),
            pltpu.VMEM((4, *tile), BF16), pltpu.VMEM((4, *tile), BF16),
            pltpu.VMEM((4, *tile), BF16), pltpu.VMEM((4, *tile), BF16),
            pltpu.VMEM((2, 4, *tile), F32),
            dma((4,)),
            dma((1,)), dma((3, 8)),
            dma((2,)), dma((2, 8)),
            dma((2,)), dma((2, 8)),
            dma((3,)), dma((3, 4)),
            dma((2,)), dma((4, 4)),
            dma((2,)), dma((2, 4, 4)),
            dma((1,)), dma((4, 2, early)),
            dma((3,)), dma((3, 4)),
            dma((2, 4)),
        ],
        compiler_params=pltpu.CompilerParams(
            collective_id=0, has_side_effects=True, vmem_limit_bytes=VMEM_LIMIT
        ),
    )(queries, keys, values, out_grad, act_exponent, grad_exponent)
    return transposed.T


def solution(mesh):
    in_specs = (
        P("dp", "tensor"),
        P("dp", "tensor"),
        P("dp", "tensor"),
        P(("dp", "tensor"), None),
        P(),
        P(),
    )
    return jax.shard_map(
        on_device, mesh=mesh, in_specs=in_specs, out_specs=P("dp", "tensor"), check_vma=False
    )
```

time: 115 us -> 108 us (0.939)
  Pallas kernels: 111 us -> 103 us
    pallas_call x1, Pallas kernels: 111 us -> 103 us  [on_device(): pl.pallas_call(kernel, name='project_grad', out_shape=jax.ShapeDtypeStruc...]
where the time goes in v3:
time: 108 us
  Pallas kernels  103 us (95%)
  local copies, waits for them, and re-layouts  2.89 us (3%)
  between operations  1.31 us (1%)
    pallas_call x1, Pallas kernels, on_device(): pl.pallas_call(kernel, name='project_grad', out_shape=jax.ShapeDtypeStruc...  103 us
    transpose x1, local copies, waits for them, and re-layouts, on_device(): return transposed.T  2.89 us

profile of v3, /device:TPU:0, one launch (start us, length us, event | category | flops | bytes accessed | tf_op | source)
XLA Modules:
  0.0 107.6 jit_solution(10987295380711130094)
XLA Ops:
  1.3 103.4 %project_grad.1 = f32[1024,512]{1,0:T(8,128)} custom-call(bf16[1024,1024]{1,0:T(8,128)(2,1)} %q_hbm.1, bf16[1024,128]{1,0:T(8,128)(2,1)} %k_hbm.1, bf16[1024,128]{1,0:T(8,128)(2,1)} %v_hbm.1, bf16[128,8192]{1,0:T(8,128)(2,1)} %g_hbm.1, s32[1]{0:T(128)S(6)} %copy.8.ae_ref, s32[1]{0:T(128)S(6)} %copy.9.ge_ref), custom_call_target="tpu_custom_call" | custom-call | tf_op jit(solution)/shard_map/project_grad/pallas_call | solution.py:339
  104.7 2.9 %copy.7 = f32[512,1024]{1,0:T(8,128)} copy(f32[512,1024]{0,1:T(8,128)} %bitcast.1) | data formatting | bytes 4194304 | tf_op jit(solution)/shard_map/transpose | solution.py:377

commit v4 on v3

--- a/solution.py
+++ b/solution.py
@@ -16,24 +16,24 @@
 OWN, OTHER = 0, 1
 
 STEPS = (
-    ("rows", 0), ("rows", 1), ("rows", 2), ("self", 0), ("self", 1), ("head", 0), ("near", 0), ("head", 1),
-    ("cols", 0), ("rows", 3), ("rows", 4), ("rows", 5), ("head", 2), ("head", 3), ("cols", 1), ("side", 0),
-    ("near", 1), ("head", 4), ("head", 5), ("cols", 2), ("rows", 6), ("rows", 7), ("head", 6), ("pass", 0),
-    ("side", 1), ("self", 2), ("near", 2), ("head", 7), ("cols", 3), ("mm", 0, 0, 1), ("mm", 0, 0, 0), ("pass", 1),
-    ("side", 2), ("self", 3), ("near", 3), ("relay", 0), ("mm", 1, 0, 1), ("pass", 2), ("side", 3), ("self", 4),
-    ("near", 4), ("mm", 2, 0, 1), ("mm", 2, 0, 0), ("pass", 3), ("side", 4), ("self", 5), ("near", 5),
-    ("mm", 3, 0, 1), ("relay", 1), ("pass", 4), ("side", 5), ("self", 6), ("near", 6), ("mm", 2, 1, 0),
-    ("mm", 1, 1, 0), ("mm", 3, 1, 0), ("mm", 0, 1, 0), ("mm", 4, 0, 1), ("mm", 4, 0, 0), ("mm", 4, 1, 0),
-    ("pass", 5), ("relay", 2), ("mm", 3, 0, 0), ("mm", 4, 1, 1), ("mm", 0, 1, 1), ("side", 6), ("self", 7),
-    ("near", 7), ("mm", 1, 1, 1), ("mm", 5, 0, 1), ("mm", 5, 1, 1), ("mm", 1, 0, 0), ("pass", 6), ("side", 7),
-    ("mm", 2, 1, 1), ("mm", 5, 1, 0), ("mm", 3, 1, 1), ("mm", 6, 0, 0), ("mm", 6, 0, 1), ("mm", 6, 1, 0),
-    ("pass", 7), ("relay", 3), ("mm", 6, 1, 1), ("mm", 0, 1, 2), ("mm", 1, 1, 2), ("mm", 4, 1, 2), ("mm", 5, 1, 2),
-    ("mm", 7, 0, 1), ("mm", 5, 0, 0), ("mm", 2, 1, 2), ("mm", 7, 1, 1), ("mm", 3, 1, 2), ("mm", 7, 1, 0),
-    ("mm", 6, 1, 2), ("mm", 7, 1, 2), ("mm", 7, 0, 0),
+    ("self", 0), ("rows", 2), ("rows", 3), ("rows", 0), ("self", 1), ("rows", 1), ("near", 0), ("near", 4),
+    ("self", 3), ("head", 0), ("head", 1), ("cols", 0), ("near", 3), ("rows", 4), ("head", 2), ("head", 3),
+    ("near", 1), ("head", 4), ("cols", 1), ("side", 3), ("rows", 5), ("head", 5), ("cols", 2), ("head", 6),
+    ("self", 4), ("side", 0), ("rows", 6), ("side", 1), ("rows", 7), ("self", 2), ("pass", 0), ("pass", 3),
+    ("head", 7), ("pass", 1), ("side", 4), ("relay", 0), ("side", 2), ("near", 2), ("mm", 0, 0, 0), ("cols", 3),
+    ("mm", 3, 0, 1), ("pass", 4), ("mm", 0, 0, 1), ("mm", 1, 0, 1), ("mm", 1, 0, 0), ("pass", 2), ("relay", 1),
+    ("near", 5), ("near", 7), ("side", 5), ("mm", 3, 1, 0), ("mm", 0, 1, 0), ("mm", 4, 0, 1), ("mm", 2, 0, 1),
+    ("mm", 1, 1, 0), ("mm", 2, 0, 0), ("self", 5), ("near", 6), ("mm", 4, 1, 0), ("self", 6), ("relay", 2),
+    ("pass", 5), ("mm", 3, 0, 0), ("mm", 3, 1, 1), ("side", 6), ("mm", 0, 1, 1), ("mm", 2, 1, 0), ("mm", 2, 1, 1),
+    ("side", 7), ("mm", 5, 1, 1), ("mm", 4, 0, 0), ("pass", 6), ("mm", 5, 1, 0), ("mm", 4, 1, 1), ("mm", 5, 0, 1),
+    ("self", 7), ("mm", 1, 1, 1), ("mm", 6, 0, 0), ("relay", 3), ("mm", 6, 0, 1), ("pass", 7), ("mm", 6, 1, 0),
+    ("mm", 0, 1, 2), ("mm", 2, 1, 2), ("mm", 3, 1, 2), ("mm", 5, 1, 2), ("mm", 5, 0, 0), ("mm", 7, 1, 0),
+    ("mm", 1, 1, 2), ("mm", 7, 0, 1), ("mm", 4, 1, 2), ("mm", 7, 1, 1), ("mm", 6, 1, 1), ("mm", 6, 1, 2),
+    ("mm", 7, 1, 2), ("mm", 7, 0, 0),
 )
-BLOCKS = ((0, 0), (0, 1), (1, 0), (1, 1), (2, 0), (2, 1), (3, 0), (3, 1))
+BLOCKS = ((0, 0), (1, 0), (2, 0), (0, 1), (1, 1), (2, 1), (3, 0), (3, 1))
 EARLY = (0, 1)
-WAY = ((1, 0), (1, 0, 0))
+WAY = ((1, 1), (1, 0, 0))
 SHIFT = (2, 1, 3, 0)
 GROUPS = ((0, 1), (2, 3)), ((0, 1), (2,), (3,))
 
@@ -58,7 +58,7 @@
 
     core_dev, side_dev, cross_dev = dev(partner_dp, t), dev(d, side_t), dev(partner_dp, side_t)
     x_devs = dev(d, low * 4 + x_up), dev(d, low * 4 + x_down)
-    z_devs = dev(yh * 8 + z_up * 2 + c, t), dev(yh * 8 + z_down * 2 + c, t)
+    z_devs = tuple(dev(yh * 8 + to * 2 + c, t) for to in (z_up, z_down, lax.rem(z + 2, 4)))
     far_dev = dev((1 - yh) * 8 + z * 2 + c, side_t)
     quarter_dev = (core_dev, side_dev, cross_dev)
     quarter_slot = ((1 - c, low), (c, 1 - low), (1 - c, 1 - low))
@@ -103,7 +103,7 @@
         g_send[2, o] = scaled(base + 2 * (1 - c) + 1 - half)
         g_send[0, o] = scaled(base + 2 * (1 - c) + half)
         g_all[o, c, low, x] = scaled(base + 2 * c + half)
-    pl.semaphore_wait(barrier, 8)
+    pl.semaphore_wait(barrier, 9)
 
     def s1_copy(k, o):
         return remote(g_send.at[k, o], g_all.at[o, c, low, x], s1_ssem.at[0], s1_rsem.at[k, o], quarter_dev[k])
@@ -224,6 +224,10 @@
                     for way in range(2):
                         zf_copy(way, stream, q).wait_recv()
                 adds += [lambda q: zf_recv.at[0, stream, q], lambda q: zf_recv.at[1, stream, q]]
+                if way2 == 2:
+                    for q in quarters:
+                        z2_copy(stream, way2, q).wait_recv()
+                    adds.append(lambda q: z2_recv.at[stream, q])
                 if not near:
                     make, key, send = last_copy, (which,), lambda q: (p_send, e_send)[which].at[q]
                 elif which == OTHER:

time: 108 us -> 106 us (0.981)
  Pallas kernels: 103 us -> 101 us
    pallas_call x1, Pallas kernels: 103 us -> 101 us  [on_device(): pl.pallas_call(kernel, name='project_grad', out_shape=jax.ShapeDtypeStruc...]
where the time goes in v4:
time: 106 us; the launch traced here: 105 us
  Pallas kernels  101 us (95%)
  local copies, waits for them, and re-layouts  2.89 us (3%)
  between operations  1.31 us (1%)
    pallas_call x1, Pallas kernels, on_device(): pl.pallas_call(kernel, name='project_grad', out_shape=jax.ShapeDtypeStruc...  101 us
    transpose x1, local copies, waits for them, and re-layouts, on_device(): return transposed.T  2.89 us

profile of v4, /device:TPU:0, one launch (start us, length us, event | category | flops | bytes accessed | tf_op | source)
XLA Modules:
  0.0 105.3 jit_solution(14252717453927255506)
XLA Ops:
  1.3 101.1 %project_grad.1 = f32[1024,512]{1,0:T(8,128)} custom-call(bf16[1024,1024]{1,0:T(8,128)(2,1)} %q_hbm.1, bf16[1024,128]{1,0:T(8,128)(2,1)} %k_hbm.1, bf16[1024,128]{1,0:T(8,128)(2,1)} %v_hbm.1, bf16[128,8192]{1,0:T(8,128)(2,1)} %g_hbm.1, s32[1]{0:T(128)S(6)} %copy.8.ae_ref, s32[1]{0:T(128)S(6)} %copy.9.ge_ref), custom_call_target="tpu_custom_call" | custom-call | tf_op jit(solution)/shard_map/project_grad/pallas_call | solution.py:343
  102.4 2.9 %copy.7 = f32[512,1024]{1,0:T(8,128)} copy(f32[512,1024]{0,1:T(8,128)} %bitcast.1) | data formatting | bytes 4194304 | tf_op jit(solution)/shard_map/transpose | solution.py:381
